TPU v7x, 32 devices: a whole 2x2x4 slice. The times are simulated.
32 devices in a mesh: island: 4 (over z), shard: 8 (over y, x, core).
Axes of the slice: x: 2, y: 2, z: 4, core: 2. Of those that a mesh axis runs over, the one named last changes fastest.
Arguments:
- weight_master: float32 [4096, 4096], P('island', 'shard'), may hold values from -6 to 6
- gain_master: float32 [4096], P(('shard', 'island')), may hold values from 0.5 to 1.5
- weight_moment: float32 [4096, 4096], P('island', 'shard'), may hold values from -0.3 to 0.3
- gain_moment: float32 [4096], P(('shard', 'island')), may hold values from -0.3 to 0.3
- attended: bfloat16 [4, 2, 768, 4096], P('island', None, 'shard'), may hold values from -6 to 6
- stream: bfloat16 [4, 2, 768, 4096], P('island', None, None, 'shard'), may hold values from -6 to 6
- targets: bfloat16 [4, 2, 768, 4096], P('island', None, None, 'shard'), may hold values from -6 to 6
Outputs:
- weight_updated: float32 [4096, 4096], P('island', 'shard')
- gain_updated: float32 [4096], P(('shard', 'island'))
- weight_velocity: float32 [4096, 4096], P('island', 'shard')
- gain_velocity: float32 [4096], P(('shard', 'island'))
All inputs are finite; a program needn't handle non-finite values.
Results may differ from a plain program's by a relative error of at most 0.0066.
Values may be sent and summed in bfloat16 or wider, within the bound.
A program may use at most 192 MiB of HBM per device.

v0:
```python
import jax
import jax.numpy as jnp
from jax import lax
from jax.sharding import PartitionSpec as P

D = 4096
STEPS = 2
norm_epsilon = 1e-05
inner_rate = 0.05
beta_one = 0.9
beta_two = 0.95
adam_epsilon = 0.3
decay_rate = 0.1
outer_rate = 0.7
outer_momentum = 0.9


def optimizer_update(param, gradient, first, second, number, decay):
    first = beta_one * first + (1.0 - beta_one) * gradient
    second = beta_two * second + (1.0 - beta_two) * gradient * gradient
    first_hat = first / (1.0 - beta_one**number)
    second_hat = second / (1.0 - beta_two**number)
    param = param - inner_rate * (first_hat / (jnp.sqrt(second_hat) + adam_epsilon) + decay * param)
    return (param, first, second)


def per_device(weight_master, gain_master, weight_moment, gain_moment, attended, stream, targets):
    islands = lax.axis_size("island")
    width_scale = D ** (-0.5)
    starts = (
        lax.all_gather(weight_master.astype(jnp.bfloat16), "island", axis=0, tiled=True),
        lax.all_gather(gain_master.astype(jnp.bfloat16), "island", axis=0, tiled=True),
    )
    weight_anchor = starts[0].astype(jnp.float32)
    gain_anchor = starts[1].astype(jnp.float32)
    weight = weight_anchor
    gain = gain_anchor
    weight_first = jnp.zeros_like(weight)
    weight_second = jnp.zeros_like(weight)
    gain_first = jnp.zeros_like(gain)
    gain_second = jnp.zeros_like(gain)
    for inner_step in range(STEPS):
        number = inner_step + 1
        rows_full = lax.all_gather(attended[0][inner_step], "shard", axis=0, tiled=True)
        weight_low = weight.astype(jnp.bfloat16)
        projected = jnp.dot(rows_full, weight_low, preferred_element_type=jnp.float32) * width_scale
        residual = stream[0][inner_step].astype(jnp.float32) + projected
        squares = lax.psum(jnp.sum(residual * residual, axis=1), "shard")
        inverse = lax.rsqrt(squares / D + norm_epsilon)[:, None]
        normed = residual * inverse * gain
        loss_low = (normed - targets[0][inner_step].astype(jnp.float32)).astype(jnp.bfloat16)
        loss_grad = lax.optimization_barrier(loss_low).astype(jnp.float32)
        scaled = loss_grad * gain
        slope = lax.psum(jnp.sum(scaled * residual, axis=1), "shard")[:, None]
        residual_grad = (
            inverse * scaled - residual * inverse * inverse * inverse * slope / D
        ).astype(jnp.bfloat16)
        weight_grad = (
            jnp.einsum("td,tf->df", rows_full, residual_grad, preferred_element_type=jnp.float32)
            * width_scale
        )
        gain_grad = jnp.sum(loss_grad * residual * inverse, axis=0)
        weight, weight_first, weight_second = optimizer_update(
            weight, weight_grad, weight_first, weight_second, number, decay_rate
        )
        gain, gain_first, gain_second = optimizer_update(
            gain, gain_grad, gain_first, gain_second, number, 0.0
        )
    weight_summed, gain_summed = (
        lax.psum_scatter(weight_anchor - weight, "island", scatter_dimension=0, tiled=True),
        lax.psum_scatter(gain_anchor - gain, "island", scatter_dimension=0, tiled=True),
    )
    weight_pseudo = weight_summed / islands
    gain_pseudo = gain_summed / islands
    weight_velocity = outer_momentum * weight_moment + weight_pseudo
    gain_velocity = outer_momentum * gain_moment + gain_pseudo
    weight_updated = weight_master - outer_rate * (weight_pseudo + outer_momentum * weight_velocity)
    gain_updated = gain_master - outer_rate * (gain_pseudo + outer_momentum * gain_velocity)
    return (weight_updated, gain_updated, weight_velocity, gain_velocity)


def solution(mesh):
    placed = (
        P("island", "shard"),
        P(("shard", "island")),
        P("island", "shard"),
        P(("shard", "island")),
        P("island", None, "shard", None),
        P("island", None, None, "shard"),
        P("island", None, None, "shard"),
    )
    return jax.shard_map(
        per_device,
        mesh=mesh,
        in_specs=placed,
        out_specs=(
            P("island", "shard"),
            P(("shard", "island")),
            P("island", "shard"),
            P(("shard", "island")),
        ),
        check_vma=False,
    )
```

profile of v0, /device:TPU:0, one launch (start us, length us, event | category | flops | bytes accessed | tf_op | source)
XLA Modules:
  0.0 416.3 jit_solution(13585546172101198673)
XLA Ops:
  7.2 0.0 all-gather.7.cloned.1.call-start
  7.2 1.9 copy.26
  9.1 1.1 convert_element_type.58
  10.3 0.0 all-gather.7.cloned.1.call-update
  10.3 0.0 all-gather.9.cloned.1.call-start
  10.4 2.7 fusion.69
  13.0 0.0 all-gather.9.cloned.1.call-update
  13.0 0.0 all-gather.11.cloned.1.call-start
  13.1 0.7 all-gather.11.cloned.1.call-update
  13.8 0.0 copy-start.5
  13.8 0.0 reduce-scatter.2.cloned.1.call-start
  13.8 2.4 fusion.68
  16.2 2.3 copy.29
  18.5 0.0 copy-done.5
  18.5 13.0 %all-gather.2 = bf16[4,1,128]{2,1,0:T(2,128)(2,1)S(1)} all-gather(bf16[1,1,128]{2,1,0:T(2,128)(2,1)S(1)} %convert_bitcast_fusion), channel_id=1, replica_groups=mesh['island'=4,'shard'=8] {'island'}, dimensions={0}, use_global_device_ids=true | all-gather | bytes 1280 | tf_op jit(solution)/shard_map/all_gather | solution.py:32
  31.5 2.6 fusion.67
  34.2 2.3 copy.30
  36.5 1.2 copy.31
  37.7 1.4 copy.32
  39.1 54.9 %all-gather.7.cloned.1.call-done = bf16[4096,512]{0,1:T(8,128)(2,1)} async-done(((bf16[1024,512]{0,1:T(8,128)(2,1)}), bf16[4096,512]{0,1:T(8,128)(2,1)}) %all-gather.7.cloned.1.call-update) | async-done | bytes 4194320 | tf_op jit(solution)/shard_map/all_gather | solution.py:31
  93.9 45.7 %all-gather.9.cloned.1.call-done = bf16[1,1,768,4096]{3,2,1,0:T(8,128)(2,1)} async-done(((bf16[1,1,96,4096]{3,2,1,0:T(8,128)(2,1)}), bf16[1,1,768,4096]{3,2,1,0:T(8,128)(2,1)}) %all-gather.9.cloned.1.call-update) | async-done | bytes 6291472 | tf_op jit(solution)/shard_map/all_gather | solution.py:44
  139.7 8.8 %multiply_reduce_fusion.1 = (f32[768]{0:T(1024)S(1)}, f32[768,512]{0,1:T(8,128)}) fusion(bf16[4096,512]{0,1:T(8,128)(2,1)} %all-gather.7.cloned.1.call-done, bf16[1,1,768,4096]{3,2,1,0:T(8,128)(2,1)} %all-gather.9.cloned.1.call-done, bf16[1,1,768,512]{2,3,1,0:T(8,128)(2,1)} %copy.29), kind=kOutput, calls=%fused_computation.51 | convolution fusion | flops 3223190784 | bytes 12848128 | tf_op jit(solution)/shard_map/dot_general | solution.py:46
  148.5 13.8 %psum.28 = f32[768]{0:T(1024)S(1)} all-reduce(f32[768]{0:T(1024)S(1)} %get-tuple-element.26), channel_id=1, replica_groups=mesh['island'=4,'shard'=8] {'shard'}, use_global_device_ids=true, to_apply=%region_1.0 | all-reduce | flops 768 | bytes 6144 | tf_op jit(solution)/shard_map/psum | solution.py:48
  162.3 0.0 copy-start.2
  162.3 2.0 fusion.33
  164.4 0.1 copy-done.2
  164.4 0.0 copy-start.4
  164.4 0.6 fusion.29
  165.1 0.3 copy-done.4
  165.3 12.7 %psum.29 = f32[768]{0:T(1024)S(1)} all-reduce(f32[768]{0:T(1024)S(1)} %get-tuple-element.15), channel_id=1, replica_groups=mesh['island'=4,'shard'=8] {'shard'}, use_global_device_ids=true, to_apply=%region_3.0 | all-reduce | flops 768 | bytes 6144 | tf_op jit(solution)/shard_map/psum | solution.py:54
  178.1 10.5 %fusion.13 = f32[512,4096]{1,0:T(8,128)} fusion(bf16[1,1,768,4096]{3,2,1,0:T(8,128)(2,1)} %all-gather.9.cloned.1.call-done, bf16[768,512]{0,1:T(8,128)(2,1)} %copy-done.4, f32[768,512]{0,1:T(8,128)} %get-tuple-element.27, f32[768]{0:T(1024)S(1)} %psum.29, f32[512]{0:T(512)S(1)} %bitcast.94, f32[768]{0:T(1024)S(1)} %add_rsqrt_fusion.1), kind=kOutput, calls=%fused_computation.19 | convolution fusion | flops 3225157632 | bytes 17047552 | tf_op jit(solution)/shard_map/td,tf->df/dot_general | solution.py:59
  188.6 0.0 all-gather.11.cloned.1.call-done
  188.6 16.5 %multiply_reduce_fusion = (f32[768]{0:T(1024)S(1)}, f32[768,512]{0,1:T(8,128)}) fusion(bf16[1,1,768,4096]{3,2,1,0:T(8,128)(2,1)} %all-gather.11.cloned.1.call-done, f32[512,4096]{1,0:T(8,128)} %fusion.13, bf16[4096,512]{0,1:T(8,128)(2,1)} %all-gather.7.cloned.1.call-done, bf16[1,1,768,512]{2,3,1,0:T(8,128)(2,1)} %copy.31), kind=kOutput, calls=%fused_computation.50 | convolution fusion | flops 3248356608 | bytes 21236736 | tf_op jit(solution)/shard_map/dot_general | solution.py:46
  205.1 12.4 %psum.30 = f32[768]{0:T(1024)S(1)} all-reduce(f32[768]{0:T(1024)S(1)} %get-tuple-element.28), channel_id=1, replica_groups=mesh['island'=4,'shard'=8] {'shard'}, use_global_device_ids=true, to_apply=%region_5.0 | all-reduce | flops 768 | bytes 6144 | tf_op jit(solution)/shard_map/psum | solution.py:48
  217.5 0.0 copy-start.1
  217.5 1.8 fusion.32
  219.3 0.0 copy-done.1
  219.3 0.0 copy-start.3
  219.3 0.6 fusion.31
  220.0 0.2 copy-done.3
  220.2 12.0 %psum.31 = f32[768]{0:T(1024)S(1)} all-reduce(f32[768]{0:T(1024)S(1)} %get-tuple-element.13), channel_id=1, replica_groups=mesh['island'=4,'shard'=8] {'shard'}, use_global_device_ids=true, to_apply=%region_8.0 | all-reduce | flops 768 | bytes 6144 | tf_op jit(solution)/shard_map/psum | solution.py:54
  232.2 22.3 %convert_subtract_fusion = f32[4096,512]{0,1:T(8,128)} fusion(bf16[4096,512]{0,1:T(8,128)(2,1)} %all-gather.7.cloned.1.call-done, f32[512,4096]{1,0:T(8,128)} %fusion.13, bf16[1,1,768,4096]{3,2,1,0:T(8,128)(2,1)} %all-gather.11.cloned.1.call-done, bf16[768,512]{0,1:T(8,128)(2,1)} %copy-done.3, f32[768,512]{0,1:T(8,128)} %get-tuple-element.29, ...), kind=kOutput, calls=%fused_computation | convolution fusion | flops 3283877888 | bytes 29630464 | tf_op jit(solution)/shard_map/td,tf->df/dot_general | solution.py:59
  254.5 0.0 reduce-scatter.2.cloned.1.call-update
  254.6 0.0 copy-start.7
  254.6 0.0 copy-start.6
  254.6 2.9 copy.25
  257.5 0.0 copy-done.7
  257.5 0.6 dynamic-slice
  258.7 12.4 %all-reduce = f32[512]{0:T(512)S(1)} all-reduce(f32[512]{0:T(512)S(1)} %subtract_subtract_fusion), channel_id=5, replica_groups=mesh['island'=4,'shard'=8] {'island'}, use_global_device_ids=true, to_apply=%region_11.0.clone | all-reduce | flops 512 | bytes 4096
  271.1 0.0 copy-done.6
  271.1 0.6 multiply_subtract_fusion.2
  271.7 127.8 %reduce-scatter.2.cloned.1.call-done = f32[1024,512]{0,1:T(8,128)} async-done(((f32[4096,512]{0,1:T(8,128)}), f32[1024,512]{0,1:T(8,128)}) %reduce-scatter.2.cloned.1.call-update) | async-done | bytes 2097168 | tf_op jit(solution)/shard_map/reduce_scatter | solution.py:70
  399.4 5.5 %multiply_add_fusion = (f32[1024,512]{0,1:T(8,128)}, f32[1024,512]{0,1:T(8,128)}) fusion(f32[1024,512]{0,1:T(8,128)} %copy.25, f32[1024,512]{0,1:T(8,128)} %reduce-scatter.2.cloned.1.call-done, f32[1024,512]{0,1:T(8,128)S(1)} %copy.26), kind=kLoop, calls=%fused_computation.25 | loop fusion | flops 3670016 | bytes 10485760 | tf_op jit(solution)/shard_map/add | solution.py:75
  404.9 0.0 copy-start
  404.9 3.0 copy.27
  407.9 0.0 copy-done
  407.9 1.8 copy.28
  (6 shorter events, 0.1 us)
Async XLA Ops:
  7.2 86.8 %all-gather.7.cloned.1.call-start = ((), (), s32[]{:S(2)}) async-start(), calls=%async_computation.1 | async-start | bytes 5242880 | tf_op jit(solution)/shard_map/all_gather | solution.py:31
  10.3 129.4 %all-gather.9.cloned.1.call-start = ((), (), s32[]{:S(2)}) async-start(), calls=%async_computation.3 | async-start | bytes 7077888 | tf_op jit(solution)/shard_map/all_gather | solution.py:44
  13.0 175.5 %all-gather.11.cloned.1.call-start = ((), (), s32[]{:S(2)}) async-start(), calls=%async_computation.4 | async-start | bytes 7077888 | tf_op jit(solution)/shard_map/all_gather | solution.py:44
  13.8 4.7 %copy-start.5 = (f32[128]{0:T(128)S(1)}, f32[128]{0:T(128)}, u32[]{:S(2)}) copy-start(f32[128]{0:T(128)} %param.8) | copy-start | bytes 1540
  13.8 385.6 %reduce-scatter.2.cloned.1.call-start = ((), (), s32[]{:S(2)}) async-start(), calls=%async_computation.2 | async-start | bytes 10485760 | tf_op jit(solution)/shard_map/reduce_scatter | solution.py:70
  162.3 2.1 copy-start.2
  164.4 0.9 copy-start.4
  217.5 1.9 copy-start.1
  219.3 0.9 copy-start.3
  254.6 2.9 copy-start.7
  254.6 16.5 %copy-start.6 = (f32[128]{0:T(128)S(1)}, f32[128]{0:T(128)}, u32[]{:S(2)}) copy-start(f32[128]{0:T(128)} %param.10) | copy-start | bytes 1540
  404.9 3.0 copy-start
Sparse Core Ops, SparseCore 0:
  10.4 83.4 all-gather.6
  95.8 43.8 all-gather.8
  142.2 45.6 all-gather.10
  254.7 144.7 reduce-scatter.1
where the time goes:
time: 417 us; the launch traced here: 416 us
  waiting for transfers between devices  229 us (55%)
  blocking collectives  76.3 us (18%)
  matrix products  58.1 us (14%)
  local copies, waits for them, and re-layouts  25.8 us (6%)
  between operations  14.5 us (3%)
  other arithmetic  12.4 us (3%)
    reduce_scatter x1, waiting for transfers between devices, per_device(): lax.psum_scatter(weight_anchor - weight, 'island', scatter_dimension=0, t...  128 us
    all_gather x1, waiting for transfers between devices, per_device(): lax.all_gather(weight_master.astype(jnp.bfloat16), 'island', axis=0, tile...  54.9 us
    all_gather x2, waiting for transfers between devices, per_device(): lax.all_gather(attended[0][inner_step], 'shard', axis=0, tiled=True)  45.7 us
    dot_general x2, matrix products, per_device(): jnp.einsum('td,tf->df', rows_full, residual_grad, preferred_element_type=...  32.8 us
    psum x2, blocking collectives, per_device(): squares = lax.psum(jnp.sum(residual * residual, axis=1), 'shard')  26.2 us
    dot_general x2, matrix products, per_device(): jnp.dot(rows_full, weight_low, preferred_element_type=jnp.float32)  25.3 us
    psum x2, blocking collectives, per_device(): slope = lax.psum(jnp.sum(scaled * residual, axis=1), 'shard')[:, None]  24.7 us
    unnamed x25, local copies, waits for them, and re-layouts  18.1 us
  transfers between devices with their start and end apart: 4, of which 3 were waited for; matrix products, arithmetic and copies ran while one was open for 10% of the time, Pallas kernels for 0%

commit v1 on v0

--- a/solution.py
+++ b/solution.py
@@ -15,6 +15,22 @@
 outer_momentum = 0.9
 
 
+def gather_around(x, axis, dim):
+    ways, here, step = (lax.axis_size(axis), lax.axis_index(axis), x.shape[dim])
+    lengths = [n * ways if d == dim else n for d, n in enumerate(x.shape)]
+    full = lax.dynamic_update_slice_in_dim(jnp.zeros(lengths, x.dtype), x, here * step, axis=dim)
+    going_up = going_down = x
+    for far in range(1, ways // 2 + 1):
+        going_up = lax.ppermute(going_up, axis, [(d, (d + 1) % ways) for d in range(ways)])
+        full = lax.dynamic_update_slice_in_dim(full, going_up, (here - far) % ways * step, axis=dim)
+        if 2 * far < ways:
+            going_down = lax.ppermute(going_down, axis, [(d, (d - 1) % ways) for d in range(ways)])
+            full = lax.dynamic_update_slice_in_dim(
+                full, going_down, (here + far) % ways * step, axis=dim
+            )
+    return full
+
+
 def optimizer_update(param, gradient, first, second, number, decay):
     first = beta_one * first + (1.0 - beta_one) * gradient
     second = beta_two * second + (1.0 - beta_two) * gradient * gradient
@@ -28,7 +44,7 @@
     islands = lax.axis_size("island")
     width_scale = D ** (-0.5)
     starts = (
-        lax.all_gather(weight_master.astype(jnp.bfloat16), "island", axis=0, tiled=True),
+        gather_around(weight_master.astype(jnp.bfloat16), "island", 0),
         lax.all_gather(gain_master.astype(jnp.bfloat16), "island", axis=0, tiled=True),
     )
     weight_anchor = starts[0].astype(jnp.float32)

time: 417 us -> 379 us (0.909)
  waiting for transfers between devices: 229 us -> 152 us
  blocking collectives: 76.3 us -> 101 us
  local copies, waits for them, and re-layouts: 25.8 us -> 35.4 us
  starting transfers between devices: 0.16 us -> 5.13 us
    all_gather x1 -> x0, waiting for transfers between devices: 54.9 us -> none  [per_device(): lax.all_gather(weight_master.astype(jnp.bfloat16), 'island', axis=0, tile...]
    all_gather x2, waiting for transfers between devices: 45.7 us -> 0.01 us  [per_device(): lax.all_gather(attended[0][inner_step], 'shard', axis=0, tiled=True)]
    all_gather x1, blocking collectives: 13 us -> 42.6 us  [per_device(): lax.all_gather(gain_master.astype(jnp.bfloat16), 'island', axis=0, tiled=...]
    ppermute x0 -> x3, waiting for transfers between devices: none -> 24.4 us  [the longest x2 24.4 us: gather_around(): lax.ppermute(going_up, axis, [(d, (d + 1) % ways) for d in range(ways)])]
    dynamic_update_slice x0 -> x3, local copies, waits for them, and re-layouts: none -> 7.01 us  [the longest x2 4.67 us: gather_around(): lax.dynamic_update_slice_in_dim(full, going_up, (here - far) % ways * ste...]
    ppermute x0 -> x3, starting transfers between devices: none -> 5.02 us  [the longest x2 3.02 us: gather_around(): lax.ppermute(going_up, axis, [(d, (d + 1) % ways) for d in range(ways)])]
  transfers between devices with their start and end apart: 4 -> 6, of which waited for: 3 -> 2; matrix products, arithmetic and copies ran while one was open for 10% -> 14% of each run, Pallas kernels for 0% -> 0%
where the time goes in v1:
time: 379 us
  waiting for transfers between devices  152 us (40%)
  blocking collectives  101 us (27%)
  matrix products  57.9 us (15%)
  local copies, waits for them, and re-layouts  35.4 us (9%)
  between operations  14.5 us (4%)
  other arithmetic  12.9 us (3%)
  starting transfers between devices  5.13 us (1%)
    reduce_scatter x1, waiting for transfers between devices, per_device(): lax.psum_scatter(weight_anchor - weight, 'island', scatter_dimension=0, t...  126 us
    all_gather x1, blocking collectives, per_device(): lax.all_gather(gain_master.astype(jnp.bfloat16), 'island', axis=0, tiled=...  42.6 us
    dot_general x2, matrix products, per_device(): jnp.einsum('td,tf->df', rows_full, residual_grad, preferred_element_type=...  32.7 us
    dot_general x2, matrix products, per_device(): jnp.dot(rows_full, weight_low, preferred_element_type=jnp.float32)  25.3 us
    ppermute x2, waiting for transfers between devices, gather_around(): lax.ppermute(going_up, axis, [(d, (d + 1) % ways) for d in range(ways)])  24.4 us
    psum x2, blocking collectives, per_device(): slope = lax.psum(jnp.sum(scaled * residual, axis=1), 'shard')[:, None]  24.2 us
    psum x2, blocking collectives, per_device(): squares = lax.psum(jnp.sum(residual * residual, axis=1), 'shard')  23.6 us
    unnamed x25, local copies, waits for them, and re-layouts  18.2 us
  transfers between devices with their start and end apart: 6, of which 2 were waited for; matrix products, arithmetic and copies ran while one was open for 14% of the time, Pallas kernels for 0%

profile of v1, /device:TPU:0, one launch (start us, length us, event | category | flops | bytes accessed | tf_op | source)
XLA Modules:
  0.0 378.7 jit_solution(17192365708915416734)
XLA Ops:
  7.2 0.0 all-gather.6.cloned.1.call-start
  7.2 2.7 fusion.69
  9.9 0.0 all-gather.6.cloned.1.call-update
  9.9 0.0 all-gather.8.cloned.1.call-start
  9.9 0.7 all-gather.8.cloned.1.call-update
  10.7 0.0 reduce-scatter.2.cloned.1.call-start
  10.7 1.9 copy.26
  12.6 2.5 broadcast_in_dim.2
  15.1 1.7 constant_dynamic-update-slice_fusion.3
  16.8 3.0 collective-permute-start
  19.9 2.0 collective-permute-start.1
  21.9 0.0 copy-start.5
  21.9 24.4 %collective-permute-done = bf16[1024,512]{0,1:T(8,128)(2,1)} collective-permute-done((bf16[1024,512]{0,1:T(8,128)(2,1)}, bf16[1024,512]{0,1:T(8,128)(2,1)}, u32[]{:S(2)}, u32[]{:S(2)}) %collective-permute-start) | collective-permute-done | bytes 1048608 | tf_op jit(solution)/shard_map/ppermute | solution.py:24
  46.2 0.0 collective-permute-start.2
  46.2 2.4 fusion.68
  48.6 2.4 copy.29
  51.0 0.0 copy-done.5
  51.0 42.6 %all-gather.2 = bf16[4,1,128]{2,1,0:T(2,128)(2,1)S(1)} all-gather(bf16[1,1,128]{2,1,0:T(2,128)(2,1)S(1)} %convert_bitcast_fusion), channel_id=1, replica_groups=mesh['island'=4,'shard'=8] {'island'}, dimensions={0}, use_global_device_ids=true | all-gather | bytes 1280 | tf_op jit(solution)/shard_map/all_gather | solution.py:48
  93.6 2.6 fusion.67
  96.2 2.3 copy.30
  98.5 1.2 copy.31
  99.7 1.4 copy.32
  101.2 2.3 constant_dynamic-update-slice_fusion.2
  103.5 0.0 collective-permute-done.1
  103.5 2.3 constant_dynamic-update-slice_fusion.1
  105.8 0.0 collective-permute-done.2
  105.8 2.3 constant_dynamic-update-slice_fusion
  108.2 0.0 all-gather.6.cloned.1.call-done
  108.2 8.8 %multiply_reduce_fusion.1 = (f32[768]{0:T(1024)S(1)}, f32[768,512]{0,1:T(8,128)}) fusion(bf16[4096,512]{0,1:T(8,128)(2,1)} %constant_dynamic-update-slice_fusion, bf16[1,1,768,4096]{3,2,1,0:T(8,128)(2,1)} %all-gather.6.cloned.1.call-done, bf16[1,1,768,512]{2,3,1,0:T(8,128)(2,1)} %copy.29), kind=kOutput, calls=%fused_computation.51 | convolution fusion | flops 3223190784 | bytes 12848128 | tf_op jit(solution)/shard_map/dot_general | solution.py:62
  117.0 11.8 %psum.28 = f32[768]{0:T(1024)S(1)} all-reduce(f32[768]{0:T(1024)S(1)} %get-tuple-element.28), channel_id=1, replica_groups=mesh['island'=4,'shard'=8] {'shard'}, use_global_device_ids=true, to_apply=%region_1.2 | all-reduce | flops 768 | bytes 6144 | tf_op jit(solution)/shard_map/psum | solution.py:64
  128.8 0.0 copy-start.2
  128.8 2.0 fusion.33
  130.8 0.1 copy-done.2
  130.9 0.0 copy-start.4
  130.9 0.6 fusion.29
  131.5 0.3 copy-done.4
  131.8 12.2 %psum.29 = f32[768]{0:T(1024)S(1)} all-reduce(f32[768]{0:T(1024)S(1)} %get-tuple-element.15), channel_id=1, replica_groups=mesh['island'=4,'shard'=8] {'shard'}, use_global_device_ids=true, to_apply=%region_3.4 | all-reduce | flops 768 | bytes 6144 | tf_op jit(solution)/shard_map/psum | solution.py:70
  144.0 10.4 %fusion.13 = f32[512,4096]{1,0:T(8,128)} fusion(bf16[1,1,768,4096]{3,2,1,0:T(8,128)(2,1)} %all-gather.6.cloned.1.call-done, bf16[768,512]{0,1:T(8,128)(2,1)} %copy-done.4, f32[768,512]{0,1:T(8,128)} %get-tuple-element.29, f32[768]{0:T(1024)S(1)} %psum.29, f32[512]{0:T(512)S(1)} %bitcast.96, f32[768]{0:T(1024)S(1)} %add_rsqrt_fusion.1), kind=kOutput, calls=%fused_computation.19 | convolution fusion | flops 3225157632 | bytes 17047552 | tf_op jit(solution)/shard_map/td,tf->df/dot_general | solution.py:75
  154.4 0.0 all-gather.8.cloned.1.call-done
  154.4 16.5 %multiply_reduce_fusion = (f32[768]{0:T(1024)S(1)}, f32[768,512]{0,1:T(8,128)}) fusion(bf16[1,1,768,4096]{3,2,1,0:T(8,128)(2,1)} %all-gather.8.cloned.1.call-done, f32[512,4096]{1,0:T(8,128)} %fusion.13, bf16[4096,512]{0,1:T(8,128)(2,1)} %constant_dynamic-update-slice_fusion, bf16[1,1,768,512]{2,3,1,0:T(8,128)(2,1)} %copy.31), kind=kOutput, calls=%fused_computation.50 | convolution fusion | flops 3248356608 | bytes 21236736 | tf_op jit(solution)/shard_map/dot_general | solution.py:62
  170.9 11.8 %psum.30 = f32[768]{0:T(1024)S(1)} all-reduce(f32[768]{0:T(1024)S(1)} %get-tuple-element.30), channel_id=1, replica_groups=mesh['island'=4,'shard'=8] {'shard'}, use_global_device_ids=true, to_apply=%region_5.6 | all-reduce | flops 768 | bytes 6144 | tf_op jit(solution)/shard_map/psum | solution.py:64
  182.7 0.0 copy-start.1
  182.7 1.8 fusion.32
  184.5 0.0 copy-done.1
  184.5 0.0 copy-start.3
  184.5 0.6 fusion.31
  185.2 0.2 copy-done.3
  185.4 12.0 %psum.31 = f32[768]{0:T(1024)S(1)} all-reduce(f32[768]{0:T(1024)S(1)} %get-tuple-element.13), channel_id=1, replica_groups=mesh['island'=4,'shard'=8] {'shard'}, use_global_device_ids=true, to_apply=%region_8.9 | all-reduce | flops 768 | bytes 6144 | tf_op jit(solution)/shard_map/psum | solution.py:70
  197.4 22.3 %convert_subtract_fusion = f32[4096,512]{0,1:T(8,128)} fusion(bf16[4096,512]{0,1:T(8,128)(2,1)} %constant_dynamic-update-slice_fusion, f32[512,4096]{1,0:T(8,128)} %fusion.13, bf16[1,1,768,4096]{3,2,1,0:T(8,128)(2,1)} %all-gather.8.cloned.1.call-done, bf16[768,512]{0,1:T(8,128)(2,1)} %copy-done.3, f32[768,512]{0,1:T(8,128)} %get-tuple-element.31, ...), kind=kOutput, calls=%fused_computation | convolution fusion | flops 3283877888 | bytes 29630464 | tf_op jit(solution)/shard_map/td,tf->df/dot_general | solution.py:75
  219.7 0.0 reduce-scatter.2.cloned.1.call-update
  219.7 0.0 copy-start.7
  219.8 0.0 copy-start.6
  219.8 2.9 copy.25
  222.7 0.0 copy-done.7
  222.7 0.6 dynamic-slice
  223.9 10.9 %all-reduce = f32[512]{0:T(512)S(1)} all-reduce(f32[512]{0:T(512)S(1)} %subtract_subtract_fusion), channel_id=5, replica_groups=mesh['island'=4,'shard'=8] {'island'}, use_global_device_ids=true, to_apply=%region_11.12.clone | all-reduce | flops 512 | bytes 4096
  234.8 0.0 copy-done.6
  234.8 0.6 multiply_subtract_fusion.2
  235.4 126.5 %reduce-scatter.2.cloned.1.call-done = f32[1024,512]{0,1:T(8,128)} async-done(((f32[4096,512]{0,1:T(8,128)}), f32[1024,512]{0,1:T(8,128)}) %reduce-scatter.2.cloned.1.call-update) | async-done | bytes 2097168 | tf_op jit(solution)/shard_map/reduce_scatter | solution.py:86
  361.8 5.5 %multiply_add_fusion = (f32[1024,512]{0,1:T(8,128)}, f32[1024,512]{0,1:T(8,128)}) fusion(f32[1024,512]{0,1:T(8,128)} %copy.25, f32[1024,512]{0,1:T(8,128)} %reduce-scatter.2.cloned.1.call-done, f32[1024,512]{0,1:T(8,128)S(1)} %copy.26), kind=kLoop, calls=%fused_computation.25 | loop fusion | flops 3670016 | bytes 10485760 | tf_op jit(solution)/shard_map/add | solution.py:91
  367.3 0.0 copy-start
  367.3 3.0 copy.27
  370.4 0.0 copy-done
  370.4 1.8 copy.28
  (6 shorter events, 0.1 us)
Async XLA Ops:
  7.2 101.0 %all-gather.6.cloned.1.call-start = ((), (), s32[]{:S(2)}) async-start(), calls=%async_computation.2 | async-start | bytes 7077888 | tf_op jit(solution)/shard_map/all_gather | solution.py:60
  9.9 144.5 %all-gather.8.cloned.1.call-start = ((), (), s32[]{:S(2)}) async-start(), calls=%async_computation.3 | async-start | bytes 7077888 | tf_op jit(solution)/shard_map/all_gather | solution.py:60
  10.7 351.2 %reduce-scatter.2.cloned.1.call-start = ((), (), s32[]{:S(2)}) async-start(), calls=%async_computation.1 | async-start | bytes 10485760 | tf_op jit(solution)/shard_map/reduce_scatter | solution.py:86
  16.8 29.4 %collective-permute-start = (bf16[1024,512]{0,1:T(8,128)(2,1)}, bf16[1024,512]{0,1:T(8,128)(2,1)}, u32[]{:S(2)}, u32[]{:S(2)}) collective-permute-start(bf16[1024,512]{0,1:T(8,128)(2,1)} %get-tuple-element.19), channel_id=1, source_target_pairs={{0,8},{8,16},{16,24},{24,0},{1,9},{9,17},{17,25},{25,1},{2,10},{10... | collective-permute-start | bytes 3145736 | tf_op jit(solution)/shard_map/ppermute | solution.py:24
  19.9 83.6 %collective-permute-start.1 = (bf16[1024,512]{0,1:T(8,128)(2,1)}, bf16[1024,512]{0,1:T(8,128)(2,1)}, u32[]{:S(2)}, u32[]{:S(2)}) collective-permute-start(bf16[1024,512]{0,1:T(8,128)(2,1)} %get-tuple-element.19), channel_id=1, source_target_pairs={{0,24},{8,0},{16,8},{24,16},{1,25},{9,1},{17,9},{25,17},{2,26},{10... | collective-permute-start | bytes 3145736 | tf_op jit(solution)/shard_map/ppermute | solution.py:27
  21.9 29.2 %copy-start.5 = (f32[128]{0:T(128)S(1)}, f32[128]{0:T(128)}, u32[]{:S(2)}) copy-start(f32[128]{0:T(128)} %param.8) | copy-start | bytes 1540
  46.2 59.6 %collective-permute-start.2 = (bf16[1024,512]{0,1:T(8,128)(2,1)}, bf16[1024,512]{0,1:T(8,128)(2,1)}, u32[]{:S(2)}, u32[]{:S(2)}) collective-permute-start(bf16[1024,512]{0,1:T(8,128)(2,1)} %collective-permute-done), channel_id=1, source_target_pairs={{0,8},{8,16},{16,24},{24,0},{1,9},{9,17},{17,25},{25,1},{2,10},{10... | collective-permute-start | bytes 3145736 | tf_op jit(solution)/shard_map/ppermute | solution.py:24
  128.8 2.1 copy-start.2
  130.9 0.9 copy-start.4
  182.7 1.9 copy-start.1
  184.5 0.9 copy-start.3
  219.7 2.9 copy-start.7
  219.8 15.0 %copy-start.6 = (f32[128]{0:T(128)S(1)}, f32[128]{0:T(128)}, u32[]{:S(2)}) copy-start(f32[128]{0:T(128)} %param.10) | copy-start | bytes 1540
  367.3 3.0 copy-start
Sparse Core Ops, SparseCore 0:
  10.0 48.1 all-gather.5
  60.6 45.3 all-gather.7
  219.9 141.9 reduce-scatter.1
